TPU v7x, 32 devices: a whole 2x2x4 slice. The times are simulated.
32 devices in a mesh: seq: 16 (over z, y, core), head: 2 (over x).
Axes of the slice: x: 2, y: 2, z: 4, core: 2. Of those that a mesh axis runs over, the one named last changes fastest.
Arguments:
- teacher: bfloat16 [1, 4096, 4096], P(None, 'seq', 'head'), may hold values from -32 to 32
- student: bfloat16 [1, 4096, 1792], P(None, 'seq', 'head'), may hold values from -32 to 32
- weights: float32 [4096], P('seq'), may hold values from 1 to 32
Outputs:
- mean_loss: float32 [], replicated
- student_grad: float32 [1, 4096, 1792], P(None, 'seq', 'head')
All inputs are finite; a program needn't handle non-finite values.
Results may differ from a plain program's by a relative error of at most 0.0011.
Values may be sent and summed in bfloat16 or wider, within the bound.
A program may use at most 128 MiB of HBM per device.

v0:
```python
import math
import jax
import jax.numpy as jnp
from jax import lax
from jax.sharding import PartitionSpec as P

TW = 256
SW = 112
HEADS = 16


def relation_scores(own_rows, key_piece, head_size):
    relations, tok_rows, columns = own_rows.shape
    head_count = columns // head_size
    queries = own_rows.reshape(relations, tok_rows, head_count, head_size)
    keys_split = key_piece.reshape(relations, key_piece.shape[1], head_count, head_size)
    return jnp.einsum(
        "rihd,rjhd->rhij", queries, keys_split, preferred_element_type=jnp.float32
    ) * (1.0 / math.sqrt(head_size))


def local(teacher, student, weights):
    relations, tok_rows, columns = teacher.shape
    head_count = columns // TW
    cycle_size = lax.axis_size("seq")
    lowest = jnp.full((relations, head_count, tok_rows), -jnp.inf, jnp.float32)
    zeroes = jnp.zeros((relations, head_count, tok_rows), jnp.float32)
    pieces = (
        lax.all_gather(teacher, "seq", axis=1, tiled=True),
        lax.all_gather(student, "seq", axis=1, tiled=True),
    )
    teach_max = lowest
    teach_sum = zeroes
    teach_cross = zeroes
    stud_max = lowest
    stud_sum = zeroes
    teach_score = relation_scores(teacher, pieces[0], TW)
    stud_score = relation_scores(student, pieces[1], SW)
    teach_top = jnp.max(teach_score, axis=-1)
    stud_top = jnp.max(stud_score, axis=-1)
    teach_exp = jnp.exp(teach_score - teach_top[..., None])
    stud_exp = jnp.exp(stud_score - stud_top[..., None])
    teach_keep = jnp.exp(teach_max - teach_top)
    stud_keep = jnp.exp(stud_max - stud_top)
    sweep_stats = (
        teach_top,
        teach_sum * teach_keep + jnp.sum(teach_exp, axis=-1),
        teach_cross * teach_keep + jnp.sum(teach_exp * (teach_score - stud_score), axis=-1),
        stud_top,
        stud_sum * stud_keep + jnp.sum(stud_exp, axis=-1),
    )
    teach_max, teach_sum, teach_cross, stud_max, stud_sum = sweep_stats
    teach_norm = teach_max + jnp.log(teach_sum)
    stud_norm = stud_max + jnp.log(stud_sum)
    divergence = teach_cross / teach_sum - teach_norm + stud_norm
    partial_loss = jnp.sum(weights[None, None, :] * divergence)
    loss_sum = lax.psum(partial_loss, ("seq", "head"))
    mean_loss = loss_sum / (relations * HEADS * tok_rows * cycle_size)
    every_teach, every_stud, every_weight = (
        lax.all_gather(teach_norm, "seq", axis=2, tiled=True),
        lax.all_gather(stud_norm, "seq", axis=2, tiled=True),
        lax.all_gather(weights, "seq", axis=0, tiled=True),
    )
    pieces = (
        lax.all_gather(teacher, "seq", axis=1, tiled=True),
        lax.all_gather(student, "seq", axis=1, tiled=True),
    )
    key_count = pieces[0].shape[1]
    teach_score = relation_scores(teacher, pieces[0], TW)
    stud_score = relation_scores(student, pieces[1], SW)
    row_part = weights[None, None, :, None] * (
        jnp.exp(stud_score - stud_norm[..., None]) - jnp.exp(teach_score - teach_norm[..., None])
    )
    col_part = every_weight[None, None, None, :] * (
        jnp.exp(stud_score - every_stud[:, :, None, :])
        - jnp.exp(teach_score - every_teach[:, :, None, :])
    )
    slope_mix = (row_part + col_part).astype(jnp.bfloat16)
    stud_keys = pieces[1].reshape(relations, key_count, head_count, SW)
    summed = jnp.einsum("rhij,rjhd->rihd", slope_mix, stud_keys, preferred_element_type=jnp.float32)
    student_grad = (summed * (1.0 / math.sqrt(SW))).reshape(relations, tok_rows, head_count * SW)
    return (mean_loss, student_grad)


def solution(mesh):
    return jax.shard_map(
        local,
        mesh=mesh,
        in_specs=(P(None, "seq", "head"), P(None, "seq", "head"), P("seq")),
        out_specs=(P(), P(None, "seq", "head")),
        check_vma=False,
    )
```

profile of v0, /device:TPU:0, one launch (start us, length us, event | category | flops | bytes accessed | tf_op | source)
XLA Modules:
  0.0 392.5 jit_solution(11814815298845756084)
XLA Ops:
  7.2 0.0 all-gather.6.cloned.1.call-start
  7.2 0.7 all-gather.6.cloned.1.call-update
  7.9 0.0 all-gather.4.cloned.1.call-start
  7.9 2.3 copy.15
  10.2 0.0 all-gather.4.cloned.1.call-update
  10.2 1.2 copy.18
  11.5 1.5 copy.22
  13.0 23.6 %all-gather = f32[16,1,256]{2,1,0:T(1,128)S(1)} all-gather(f32[1,1,256]{2,1,0:T(1,128)} %bitcast.61), channel_id=1, replica_groups=mesh['seq'=16,'head'=2] {'seq'}, dimensions={0}, use_global_device_ids=true | all-gather | bytes 17408 | tf_op jit(solution)/shard_map/all_gather | solution.py:62
  36.6 44.1 %all-gather.6.cloned.1.call-done = bf16[1,4096,896]{2,1,0:T(8,128)(2,1)} async-done(((bf16[1,256,896]{2,1,0:T(8,128)(2,1)}), bf16[1,4096,896]{2,1,0:T(8,128)(2,1)}) %all-gather.6.cloned.1.call-update) | async-done | bytes 7340048 | tf_op jit(solution)/shard_map/all_gather | solution.py:30
  80.7 10.8 %copy.19 = bf16[1,4096,896]{1,2,0:T(8,128)(2,1)} copy(bf16[1,4096,896]{2,1,0:T(8,128)(2,1)} %all-gather.6.cloned.1.call-done) | data formatting | bytes 14680064 | tf_op jit(solution)/shard_map/all_gather | solution.py:30
  91.5 120.0 %all-gather.4.cloned.1.call-done = bf16[1,4096,2048]{1,2,0:T(8,128)(2,1)} async-done(((bf16[1,256,2048]{1,2,0:T(8,128)(2,1)}), bf16[1,4096,2048]{1,2,0:T(8,128)(2,1)}) %all-gather.4.cloned.1.call-update) | async-done | bytes 16777232 | tf_op jit(solution)/shard_map/all_gather | solution.py:29
  211.6 19.3 %multiply_reduce_fusion.2 = (f32[8,256]{1,0:T(8,128)S(1)}, f32[8,256,4096]{2,1,0:T(8,128)}) fusion(bf16[4096,8,256]{0,2,1:T(8,128)(2,1)} %bitcast.51, bf16[256,8,256]{2,1,0:T(8,128)(2,1)S(1)} %bitcast.54), kind=kOutput, calls=%fused_computation.6 | convolution fusion | flops 4311742464 | bytes 51388416 | tf_op jit(solution)/shard_map/rihd,rjhd->rhij/dot_general | solution.py:17
  230.8 29.6 %fusion = (f32[8,256]{1,0:T(8,128)S(1)}, f32[8,256]{1,0:T(8,128)S(1)}, f32[8,256]{1,0:T(8,128)S(1)}, f32[8,256,4096]{2,1,0:T(8,128)}) fusion(f32[8,256,4096]{2,1,0:T(8,128)} %get-tuple-element.15, f32[8,256]{1,0:T(8,128)S(1)} %get-tuple-element.14, bf16[256,8,112]{0,2,1:T(8,128)(2,1)S(1)} %bitcast.57, bf16[4096,8,112]{0,2,1:T(8,128)(2,1)} %bitcast.52), kind=kOutput, calls=%fused_computation.4 | convolution fusion | flops 1946150912 | bytes 74940416 | tf_op jit(solution)/shard_map/rihd,rjhd->rhij/dot_general | solution.py:17
  260.5 0.0 copy-start
  260.5 14.0 %exponential_reduce_fusion = f32[8,256]{1,0:T(8,128)S(1)} fusion(f32[8,256,4096]{2,1,0:T(8,128)} %get-tuple-element.16, f32[8,256]{1,0:T(8,128)S(1)} %get-tuple-element.10), kind=kLoop, calls=%fused_computation.1 | loop fusion | flops 25163776 | bytes 33570816 | tf_op jit(solution)/shard_map/reduce_sum | solution.py:50
  274.5 0.0 copy-done
  274.6 0.6 multiply_reduce_fusion.3
  275.2 38.5 %psum.7 = f32[]{:T(128)} all-reduce(f32[]{:T(128)} %get-tuple-element.11), channel_id=1, replica_groups=mesh['seq'=16,'head'=2] {'seq','head'}, use_global_device_ids=true, to_apply=%region_6.0 | all-reduce | flops 1 | bytes 8 | tf_op jit(solution)/shard_map/psum | solution.py:57
  313.7 21.6 %all_gather.21 = f32[1,8,4096]{2,1,0:T(8,128)S(1)} all-gather(f32[1,8,256]{2,1,0:T(8,128)S(1)} %fusion.6), channel_id=1, replica_groups=mesh['seq'=16,'head'=2] {'seq'}, dimensions={2}, use_global_device_ids=true | all-gather | bytes 139264 | tf_op jit(solution)/shard_map/all_gather | solution.py:60
  335.3 17.9 %all_gather.20 = f32[1,8,4096]{2,1,0:T(8,128)S(1)} all-gather(f32[1,8,256]{2,1,0:T(8,128)S(1)} %fusion.10), channel_id=1, replica_groups=mesh['seq'=16,'head'=2] {'seq'}, dimensions={2}, use_global_device_ids=true | all-gather | bytes 139264 | tf_op jit(solution)/shard_map/all_gather | solution.py:61
  353.2 29.4 %fusion.2 = f32[8,256,112]{1,2,0:T(8,128)S(1)} fusion(bf16[4096,8,112]{0,2,1:T(8,128)(2,1)} %bitcast.53, f32[8,256,4096]{2,1,0:T(8,128)} %get-tuple-element.16, f32[8,256,4096]{2,1,0:T(8,128)} %get-tuple-element.15, f32[8,4096]{1,0:T(8,128)S(1)} %bitcast.58, f32[8,4096]{1,0:T(8,128)S(1)} %bitcast.59, f32[4096]{0:T(1024)S(1)} %bitcast.60, ...), kind=kOutput, calls=%fused_computation.8 | convolution fusion | flops 1979940864 | bytes 75662336 | tf_op jit(solution)/shard_map/rhij,rjhd->rihd/dot_general | solution.py:80
  382.7 1.2 copy.20
  (2 shorter events, 0.0 us)
Async XLA Ops:
  7.2 73.6 %all-gather.6.cloned.1.call-start = ((), (), s32[]{:S(2)}) async-start(), calls=%async_computation.1 | async-start | bytes 7798784 | tf_op jit(solution)/shard_map/all_gather | solution.py:30
  7.9 203.7 %all-gather.4.cloned.1.call-start = ((), (), s32[]{:S(2)}) async-start(), calls=%async_computation | async-start | bytes 17825792 | tf_op jit(solution)/shard_map/all_gather | solution.py:29
  260.5 14.1 %copy-start = (f32[256]{0:T(256)S(1)}, f32[256]{0:T(256)}, u32[]{:S(2)}) copy-start(f32[256]{0:T(256)} %param.5) | copy-start | bytes 3076
Sparse Core Ops, SparseCore 0:
  10.3 70.4 all-gather.5
  82.9 128.6 all-gather.3
where the time goes:
time: 393 us
  waiting for transfers between devices  165 us (42%)
  blocking collectives  102 us (26%)
  matrix products  78.3 us (20%)
  local copies, waits for them, and re-layouts  17.1 us (4%)
  between operations  15.9 us (4%)
  other arithmetic  14.7 us (4%)
    all_gather x1, waiting for transfers between devices, local(): lax.all_gather(teacher, 'seq', axis=1, tiled=True)  120 us
    dot_general x2, matrix products, relation_scores(): jnp.einsum('rihd,rjhd->rhij', queries, keys_split, preferred_element_type...  48.9 us
    all_gather x1, waiting for transfers between devices, local(): lax.all_gather(student, 'seq', axis=1, tiled=True)  44.1 us
    psum x1, blocking collectives, local(): loss_sum = lax.psum(partial_loss, ('seq', 'head'))  38.5 us
    dot_general x1, matrix products, local(): jnp.einsum('rhij,rjhd->rihd', slope_mix, stud_keys, preferred_element_typ...  29.4 us
    all_gather x1, blocking collectives, local(): lax.all_gather(weights, 'seq', axis=0, tiled=True)  23.6 us
    all_gather x1, blocking collectives, local(): lax.all_gather(teach_norm, 'seq', axis=2, tiled=True)  21.6 us
    all_gather x1, blocking collectives, local(): lax.all_gather(stud_norm, 'seq', axis=2, tiled=True)  17.9 us
  transfers between devices with their start and end apart: 2, of which 2 were waited for; matrix products, arithmetic and copies ran while one was open for 4% of the time, Pallas kernels for 0%

commit v1 on v0

--- a/solution.py
+++ b/solution.py
@@ -7,6 +7,11 @@
 TW = 256
 SW = 112
 HEADS = 16
+
+
+def gather_blocks(array, name, along):
+    blocks = lax.all_gather(array, name)
+    return jnp.concatenate(blocks, axis=along)
 
 
 def relation_scores(own_rows, key_piece, head_size):
@@ -25,10 +30,7 @@
     cycle_size = lax.axis_size("seq")
     lowest = jnp.full((relations, head_count, tok_rows), -jnp.inf, jnp.float32)
     zeroes = jnp.zeros((relations, head_count, tok_rows), jnp.float32)
-    pieces = (
-        lax.all_gather(teacher, "seq", axis=1, tiled=True),
-        lax.all_gather(student, "seq", axis=1, tiled=True),
-    )
+    pieces = (gather_blocks(teacher, "seq", 1), lax.all_gather(student, "seq", axis=1, tiled=True))
     teach_max = lowest
     teach_sum = zeroes
     teach_cross = zeroes

time: 393 us -> 424 us (1.079)
  local copies, waits for them, and re-layouts: 17.1 us -> 33.5 us
  matrix products: 78.3 us -> 93.8 us
    all_gather x1, waiting for transfers between devices: 120 us -> 0.01 us  [local(): lax.all_gather(teacher, 'seq', axis=1, tiled=True)]
    all_gather x0 -> x1, waiting for transfers between devices: none -> 117 us  [gather_blocks(): blocks = lax.all_gather(array, name)]
    unnamed x6 -> x7, local copies, waits for them, and re-layouts: 6.25 us -> 22.7 us
    dot_general x2, matrix products: 48.9 us -> 62 us  [relation_scores(): jnp.einsum('rihd,rjhd->rhij', queries, keys_split, preferred_element_type...]
  transfers between devices with their start and end apart: 2 -> 3, of which waited for: 2 -> 2; matrix products, arithmetic and copies ran while one was open for 4% -> 26% of each run, Pallas kernels for 0% -> 0%
where the time goes in v1:
time: 424 us; the launch traced here: 423 us
  waiting for transfers between devices  161 us (38%)
  blocking collectives  104 us (25%)
  matrix products  93.8 us (22%)
  local copies, waits for them, and re-layouts  33.5 us (8%)
  between operations  15.6 us (4%)
  other arithmetic  14.9 us (4%)
    all_gather x1, waiting for transfers between devices, gather_blocks(): blocks = lax.all_gather(array, name)  117 us
    dot_general x2, matrix products, relation_scores(): jnp.einsum('rihd,rjhd->rhij', queries, keys_split, preferred_element_type...  62 us
    all_gather x1, waiting for transfers between devices, local(): lax.all_gather(student, 'seq', axis=1, tiled=True)  43.2 us
    psum x1, blocking collectives, local(): loss_sum = lax.psum(partial_loss, ('seq', 'head'))  38.8 us
    dot_general x1, matrix products, local(): jnp.einsum('rhij,rjhd->rihd', slope_mix, stud_keys, preferred_element_typ...  31.8 us
    all_gather x1, blocking collectives, local(): lax.all_gather(weights, 'seq', axis=0, tiled=True)  23.8 us
    unnamed x7, local copies, waits for them, and re-layouts  22.7 us
    all_gather x1, blocking collectives, local(): lax.all_gather(teach_norm, 'seq', axis=2, tiled=True)  22.2 us
  transfers between devices with their start and end apart: 3, of which 2 were waited for; matrix products, arithmetic and copies ran while one was open for 26% of the time, Pallas kernels for 0%

profile of v1, /device:TPU:0, one launch (start us, length us, event | category | flops | bytes accessed | tf_op | source)
XLA Modules:
  0.0 423.3 jit_solution(6948077724405835987)
XLA Ops:
  7.2 0.0 all-gather.6.cloned.1.call-start
  7.2 0.7 all-gather.6.cloned.1.call-update
  7.9 0.0 all-gather.10.cloned.1.call-start
  7.9 0.7 all-gather.10.cloned.1.call-update
  8.6 0.0 all-gather.8.cloned.1.call-start
  8.7 2.3 copy.22
  11.0 0.0 all-gather.8.cloned.1.call-update
  11.0 1.2 copy.20
  12.2 1.5 copy.27
  13.8 23.8 %all-gather.1 = f32[16,1,256]{2,1,0:T(1,128)S(1)} all-gather(f32[1,1,256]{2,1,0:T(1,128)} %bitcast.66), channel_id=1, replica_groups=mesh['seq'=16,'head'=2] {'seq'}, dimensions={0}, use_global_device_ids=true | all-gather | bytes 17408 | tf_op jit(solution)/shard_map/all_gather | solution.py:64
  37.6 43.2 %all-gather.6.cloned.1.call-done = bf16[1,4096,896]{2,1,0:T(8,128)(2,1)} async-done(((bf16[1,256,896]{2,1,0:T(8,128)(2,1)}), bf16[1,4096,896]{2,1,0:T(8,128)(2,1)}) %all-gather.6.cloned.1.call-update) | async-done | bytes 7340048 | tf_op jit(solution)/shard_map/all_gather | solution.py:33
  80.7 10.8 %copy.21 = bf16[1,4096,896]{1,2,0:T(8,128)(2,1)} copy(bf16[1,4096,896]{2,1,0:T(8,128)(2,1)} %all-gather.6.cloned.1.call-done) | data formatting | bytes 14680064 | tf_op jit(solution)/shard_map/all_gather | solution.py:33
  91.5 116.6 %all-gather.10.cloned.1.call-done = bf16[16,256,2048]{2,1,0:T(8,128)(2,1)} async-done(((bf16[1,256,2048]{2,1,0:T(8,128)(2,1)}), bf16[16,256,2048]{2,1,0:T(8,128)(2,1)}) %all-gather.10.cloned.1.call-update) | async-done | bytes 16777232 | tf_op jit(solution)/shard_map/all_gather | solution.py:13
  208.1 16.4 %copy.28 = bf16[512,8,8,256]{3,2,1,0:T(8,128)(2,1)} copy(bf16[512,8,8,256]{3,1,2,0:T(8,128)(2,1)} %bitcast.55) | data formatting | bytes 33554432
  224.6 31.9 %multiply_reduce_fusion.1 = (f32[8,256]{1,0:T(8,128)S(1)}, f32[8,256,4096]{2,1,0:T(8,128)}) fusion(bf16[4096,8,256]{2,1,0:T(8,128)(2,1)} %bitcast.54, bf16[256,8,256]{2,1,0:T(8,128)(2,1)S(1)} %bitcast.59), kind=kOutput, calls=%fused_computation.5 | convolution fusion | flops 4311742464 | bytes 51388416 | tf_op jit(solution)/shard_map/rihd,rjhd->rhij/dot_general | solution.py:22
  256.4 30.1 %fusion = (f32[8,256]{1,0:T(8,128)S(1)}, f32[8,256]{1,0:T(8,128)S(1)}, f32[8,256]{1,0:T(8,128)S(1)}, f32[8,256,4096]{2,1,0:T(8,128)}) fusion(f32[8,256,4096]{2,1,0:T(8,128)} %get-tuple-element.15, f32[8,256]{1,0:T(8,128)S(1)} %get-tuple-element.14, bf16[256,8,112]{0,2,1:T(8,128)(2,1)S(1)} %bitcast.62, bf16[4096,8,112]{0,2,1:T(8,128)(2,1)} %bitcast.57), kind=kOutput, calls=%fused_computation.4 | convolution fusion | flops 1946150912 | bytes 74940416 | tf_op jit(solution)/shard_map/rihd,rjhd->rhij/dot_general | solution.py:22
  286.6 0.0 copy-start
  286.6 14.2 %exponential_reduce_fusion = f32[8,256]{1,0:T(8,128)S(1)} fusion(f32[8,256,4096]{2,1,0:T(8,128)} %get-tuple-element.16, f32[8,256]{1,0:T(8,128)S(1)} %get-tuple-element.10), kind=kLoop, calls=%fused_computation.1 | loop fusion | flops 25163776 | bytes 33570816 | tf_op jit(solution)/shard_map/reduce_sum | solution.py:52
  300.8 19.5 %all_gather.27 = f32[1,8,4096]{2,1,0:T(8,128)S(1)} all-gather(f32[1,8,256]{2,1,0:T(8,128)S(1)} %fusion.15), channel_id=1, replica_groups=mesh['seq'=16,'head'=2] {'seq'}, dimensions={2}, use_global_device_ids=true | all-gather | bytes 139264 | tf_op jit(solution)/shard_map/all_gather | solution.py:63
  320.3 22.2 %all_gather.28 = f32[1,8,4096]{2,1,0:T(8,128)S(1)} all-gather(f32[1,8,256]{2,1,0:T(8,128)S(1)} %fusion.11), channel_id=1, replica_groups=mesh['seq'=16,'head'=2] {'seq'}, dimensions={2}, use_global_device_ids=true | all-gather | bytes 139264 | tf_op jit(solution)/shard_map/all_gather | solution.py:62
  342.6 0.0 copy-done
  342.6 0.6 multiply_reduce_fusion.3
  343.2 0.0 all-gather.8.cloned.1.call-done
  343.2 31.8 %fusion.6 = f32[8,256,112]{1,2,0:T(8,128)S(1)} fusion(bf16[4096,8,112]{0,2,1:T(8,128)(2,1)} %bitcast.58, f32[8,256,4096]{2,1,0:T(8,128)} %get-tuple-element.16, f32[8,4096]{1,0:T(8,128)S(1)} %bitcast.64, f32[8,4096]{1,0:T(8,128)S(1)} %bitcast.63, f32[4096]{0:T(1024)S(1)} %bitcast.65, f32[8,256]{1,0:T(8,128)S(1)} %get-tuple-element.13, ...), kind=kOutput, calls=%fused_computation.11 | convolution fusion | flops 6274908160 | bytes 59933696 | tf_op jit(solution)/shard_map/rhij,rjhd->rihd/dot_general | solution.py:82
  375.0 1.2 copy.25
  376.2 38.8 %psum.7 = f32[]{:T(128)} all-reduce(f32[]{:T(128)} %get-tuple-element.11), channel_id=1, replica_groups=mesh['seq'=16,'head'=2] {'seq','head'}, use_global_device_ids=true, to_apply=%region_6.0 | all-reduce | flops 1 | bytes 8 | tf_op jit(solution)/shard_map/psum | solution.py:59
  (2 shorter events, 0.0 us)
Async XLA Ops:
  7.2 73.6 %all-gather.6.cloned.1.call-start = ((), (), s32[]{:S(2)}) async-start(), calls=%async_computation | async-start | bytes 7798784 | tf_op jit(solution)/shard_map/all_gather | solution.py:33
  7.9 200.2 %all-gather.10.cloned.1.call-start = ((), (), s32[]{:S(2)}) async-start(), calls=%async_computation.2 | async-start | bytes 17825792 | tf_op jit(solution)/shard_map/all_gather | solution.py:13
  8.6 334.5 %all-gather.8.cloned.1.call-start = ((), (), s32[]{:S(2)}) async-start(), calls=%async_computation.1 | async-start | bytes 17825792 | tf_op jit(solution)/shard_map/all_gather | solution.py:67
  286.6 56.0 %copy-start = (f32[256]{0:T(256)S(1)}, f32[256]{0:T(256)}, u32[]{:S(2)}) copy-start(f32[256]{0:T(256)} %param.5) | copy-start | bytes 3076
Sparse Core Ops, SparseCore 0:
  10.3 70.4 all-gather.5
  82.9 125.1 all-gather.9
  210.3 129.3 all-gather.7
